TPU v7x, 32 devices: a whole 2x2x4 slice. The times are simulated.
32 devices in a mesh: gx: 16 (over z, x, core), gy: 2 (over y).
Axes of the slice: x: 2, y: 2, z: 4, core: 2. Of those that a mesh axis runs over, the one named last changes fastest.
Arguments:
- velocity: float32 [256, 256, 512], P('gx', 'gy'), may hold values from -24 to 24
- viscosity: float32 [256], P('gx'), may hold values from 1000 to 8000
- marker_forces: bfloat16 [4096, 16], P(('gx', 'gy')), may hold values from -18 to 18
- spread_weights: bfloat16 [4096, 16, 2048], P(('gx', 'gy')), may hold values from -1.5 to 1.5
- block_owner: int32 [4096, 1], P(('gx', 'gy')), may hold values from 0 to 31; in each aligned block of 128 rows (0 to 127, 128 to 255, ...) at most 8 rows name the same one
- tile_slot: int32 [4096], P(('gx', 'gy')), may hold values from 0 to 511
Outputs:
- relaxed: float32 [256, 256, 512], P('gx', 'gy')
Inputs may be any that keep to these rules, and one draw needn't show every extreme that they name: `block_owner`: among the 128 blocks held by one device, no owner is named by more than 8 of them.
All inputs are finite; a program needn't handle non-finite values.
Results may differ from a plain program's by a relative error of at most 0.0013.
Values may be sent and summed in bfloat16 or wider, within the bound.
A program may use at most 128 MiB of HBM per device.

v0:
```python
import jax
import jax.numpy as jnp
from jax import lax
from jax.sharding import PartitionSpec as P


def passed_along(x, axis, by):
    length = lax.axis_size(axis)
    pairs = [(i, i + by) for i in range(length) if 0 <= i + by < length]
    return lax.ppermute(x, axis, pairs)


def thomas(below_diag, main_diag, above_diag, right_side):
    count_rows = right_side.shape[0]
    pivot_value = main_diag[0]
    ratios = [above_diag[0] / pivot_value]
    values = [right_side[0] / pivot_value]
    for row_index in range(1, count_rows):
        pivot_value = main_diag[row_index] - below_diag[row_index] * ratios[-1]
        ratios.append(above_diag[row_index] / pivot_value)
        values.append((right_side[row_index] - below_diag[row_index] * values[-1]) / pivot_value)
    result = [values[-1]]
    for row_index in range(count_rows - 2, -1, -1):
        result.append(values[row_index] - ratios[row_index] * result[-1])
    return jnp.stack(result[::-1])


def per_device(velocity, viscosity, marker_forces, spread_weights, block_owner, tile_slot):
    cells_x, cells_y, cells_z = velocity.shape
    line_count = cells_y * cells_z
    grid_x = lax.axis_size("gx")
    grid_y = lax.axis_size("gy")
    devices = grid_x * grid_y
    tile_values = jnp.einsum(
        "bm,bmt->bt", marker_forces, spread_weights, preferred_element_type=jnp.float32
    ).astype(jnp.bfloat16)
    block_count = tile_values.shape[0]
    capacity = max(2, 2 * block_count // devices)
    segment = tile_values.shape[1] // cells_x
    owner_dev = block_owner[:, 0]
    matches = (owner_dev[:, None] == jnp.arange(devices, dtype=jnp.int32)[None, :]).astype(
        jnp.int32
    )
    ranking = jnp.sum(jnp.cumsum(matches, axis=0) * matches, axis=1) - 1
    target = owner_dev * capacity + ranking
    select = target[None, :] == jnp.arange(devices * capacity, dtype=jnp.int32)[:, None]
    outgoing = jnp.dot(
        select.astype(jnp.bfloat16), tile_values, preferred_element_type=jnp.float32
    ).astype(jnp.bfloat16)
    out_slots = (
        jnp.sum(jnp.where(select, tile_slot[None, :], 0), axis=1)
        + jnp.sum(select.astype(jnp.int32), axis=1)
        - 1
    )
    arrived, arrived_slots = (
        lax.all_to_all(
            outgoing.reshape(devices, capacity, -1),
            ("gx", "gy"),
            split_axis=0,
            concat_axis=0,
            tiled=True,
        ),
        lax.all_to_all(
            out_slots.reshape(devices, capacity),
            ("gx", "gy"),
            split_axis=0,
            concat_axis=0,
            tiled=True,
        ),
    )
    positions = line_count // segment
    placing = (
        arrived_slots.reshape(-1)[None, :] == jnp.arange(positions, dtype=jnp.int32)[:, None]
    ).astype(jnp.bfloat16)
    force_field = jnp.einsum(
        "pr,rxs->xps",
        placing,
        arrived.reshape(-1, cells_x, segment),
        preferred_element_type=jnp.float32,
    )
    right_side = velocity.reshape(cells_x, line_count) + force_field.reshape(cells_x, line_count)
    inner_rows = cells_x - 1
    below_diag = -viscosity
    above_diag = -viscosity
    main_diag = 1.0 + 2.0 * viscosity
    interior = thomas(
        below_diag[:inner_rows],
        main_diag[:inner_rows],
        above_diag[:inner_rows],
        right_side[:inner_rows],
    )
    unit_columns = (
        jnp.zeros((inner_rows, 2), jnp.float32).at[0, 0].add(1.0).at[inner_rows - 1, 1].add(1.0)
    )
    spikes = thomas(
        below_diag[:inner_rows], main_diag[:inner_rows], above_diag[:inner_rows], unit_columns
    )
    first_spike = spikes[:, 0]
    last_spike = spikes[:, 1]
    below_first = below_diag[0]
    above_inner = above_diag[inner_rows - 1]
    below_sep = below_diag[inner_rows]
    main_sep = main_diag[inner_rows]
    above_sep = above_diag[inner_rows]
    position = lax.axis_index("gx")
    handed = jnp.stack([below_first * first_spike[0], above_inner * last_spike[0]])
    next_first, next_scalars = passed_along((interior[0], handed), "gx", -1)
    lower_coef = jnp.where(
        position > 0, -below_sep * below_first * first_spike[inner_rows - 1], 0.0
    )
    center_coef = (
        main_sep
        - below_sep * above_inner * last_spike[inner_rows - 1]
        - above_sep * next_scalars[0]
    )
    upper_coef = -above_sep * next_scalars[1]
    reduced_side = (
        right_side[inner_rows] - below_sep * interior[inner_rows - 1] - above_sep * next_first
    )
    coefficients = jnp.stack([lower_coef, center_coef, upper_coef])
    split_coef = lax.all_gather(coefficients, "gx", axis=0, tiled=True).reshape(-1, 3)
    sides = lax.all_to_all(
        reduced_side.reshape(1, grid_x, -1), "gx", split_axis=1, concat_axis=0, tiled=True
    )[:, 0, :]
    separators = lax.linalg.tridiagonal_solve(
        split_coef[:, 0], split_coef[:, 1], split_coef[:, 2], sides
    )
    earlier = jnp.concatenate([jnp.zeros_like(separators[:1]), separators[:-1]], axis=0)
    solved_pairs = jnp.stack([separators, earlier])
    returned = lax.all_to_all(solved_pairs, "gx", split_axis=1, concat_axis=2, tiled=True)
    own_value = returned[0, 0]
    previous = returned[1, 0]
    inner_part = (
        interior
        - below_first * previous[None, :] * first_spike[:, None]
        - above_inner * own_value[None, :] * last_spike[:, None]
    )
    updated = jnp.concatenate([inner_part, own_value[None, :]], axis=0)
    return updated.reshape(velocity.shape)


def solution(mesh):
    placed = (
        P("gx", "gy", None),
        P("gx"),
        P(("gx", "gy"), None),
        P(("gx", "gy"), None, None),
        P(("gx", "gy"), None),
        P(("gx", "gy")),
    )
    return jax.shard_map(
        per_device, mesh=mesh, in_specs=placed, out_specs=P("gx", "gy", None), check_vma=False
    )
```

profile of v0, /device:TPU:0, one launch (start us, length us, event | category | flops | bytes accessed | tf_op | source)
XLA Modules:
  0.0 286.4 jit_solution(17958586952579366199)
XLA Ops:
  0.0 0.7 fusion.7
  0.9 0.8 select_reduce_fusion.1
  2.4 0.8 convert_reduce_fusion
  3.2 0.7 sub.3650
  3.9 7.3 %all-to-all-start.1 = ((s32[32,1,8]{2,1,0:T(1,128)}), s32[32,1,8]{2,1,0:T(1,128)S(1)}, u32[]{:S(2)}, u32[]{:S(2)}) async-start(s32[32,1,8]{2,1,0:T(1,128)} %bitcast.4), calls=%async_computation.1 | async-start | bytes 32768 | tf_op jit(solution)/shard_map/all_to_all | solution.py:63
  11.3 0.8 copy.18
  12.1 4.8 %fusion.70 = bf16[128,1,2048]{2,1,0:T(2,128)(2,1)S(1)} fusion(bf16[128,16,1]{1,2,0:T(2,128)(2,1)S(1)} %copy.18, bf16[128,16,2048]{2,1,0:T(8,128)(2,1)} %param.13), kind=kOutput, calls=%fused_computation.197 | convolution fusion | flops 8388608 | bytes 8916992 | tf_op jit(solution)/shard_map/bm,bmt->bt/dot_general | solution.py:34
  16.9 1.5 fusion
  18.4 5.8 %all-to-all-start = ((bf16[32,8,2048]{2,1,0:T(8,128)(2,1)}), bf16[32,8,2048]{2,1,0:T(8,128)(2,1)S(1)}, u32[]{:S(2)}, u32[]{:S(2)}) async-start(bf16[32,8,2048]{2,1,0:T(8,128)(2,1)} %fusion), calls=%async_computation | async-start | bytes 2097152 | tf_op jit(solution)/shard_map/all_to_all | solution.py:56
  24.3 0.7 fusion.69
  25.0 0.7 fusion.68
  52.6 8.7 %subtract_divide_fusion.29 = (f32[1,2]{0,1:T(2,128)S(1)}, f32[1,2]{0,1:T(2,128)S(1)}, f32[1,2]{0,1:T(2,128)S(1)}, f32[1,2]{0,1:T(2,128)S(1)}, f32[1,2]{0,1:T(2,1...) fusion(f32[]{:T(128)S(6)} %sub.3676, ...), kind=kLoop, calls=%fused_computation.160 | loop fusion | flops 80 | bytes 220 | tf_op jit(solution)/shard_map/div | solution.py:21
  61.3 1.2 multiply_subtract_fusion.31
  65.7 1.3 collective-permute-start.1
  68.7 6.6 %copy.20 = f32[2,8,128,512]{3,1,2,0:T(8,128)} copy(f32[2,8,128,512]{3,2,1,0:T(8,128)} %bitcast.267) | data formatting | bytes 8388608
  81.8 34.9 %all-reduce.1 = f32[48]{0:T(128)S(1)} all-reduce(f32[48]{0:T(128)S(1)} %maximum_dynamic-update-slice_fusion), channel_id=1, replica_groups=mesh['gx'=16,'gy'=2] {'gx'}, use_global_device_ids=true, to_apply=%add.1 | all-reduce | flops 48 | bytes 384
  117.5 0.7 fusion.63
  135.0 0.7 fusion.62
  148.3 0.7 reduce.66
  149.3 2.7 convolution_bitcast_fusion
  152.1 5.3 %copy.16 = f32[16,512,128]{2,1,0:T(8,128)} copy(f32[16,512,128]{1,2,0:T(8,128)} %convolution_bitcast_fusion) | data formatting | bytes 8388608 | tf_op jit(solution)/shard_map/pr,rxs->xps/transpose | solution.py:75
  157.4 6.0 %bitcast_add_fusion = f32[16,65536]{1,0:T(8,128)S(1)} fusion(f32[16,65536]{1,0:T(8,128)} %bitcast.265, f32[2,8,512,128]{3,2,1,0:T(8,128)} %bitcast.266), kind=kLoop, calls=%fused_computation | loop fusion | flops 1048576 | bytes 12582912 | tf_op jit(solution)/shard_map/add | solution.py:81
  163.4 17.6 %fusion.39 = (f32[65536]{0:T(1024)}, f32[1,65536]{1,0:T(1,128)S(1)}, f32[1,65536]{1,0:T(1,128)S(1)}, f32[1,65536]{1,0:T(1,128)S(1)}, f32[1,65536]{1,0:T(1,128)S(...) fusion(f32[]{:T(128)S(6)} %div.2722, ...), kind=kLoop, calls=%fused_computation.181 | loop fusion | flops 2949120 | bytes 8126584 | tf_op jit(solution)/shard_map/sub | solution.py:24
  181.0 3.3 %fusion.61 = (f32[1,65536]{1,0:T(1,128)S(1)}, f32[1,65536]{1,0:T(1,128)S(1)}, f32[1,65536]{1,0:T(1,128)S(1)}, f32[1,65536]{1,0:T(1,128)S(1)}, f32[1,65536]{1,0:T...) fusion(f32[16,65536]{1,0:T(8,128)S(1)} %bitcast_add_fusion), kind=kLoop, calls=%fused_computation.188 | loop fusion | bytes 7864320 | tf_op jit(solution)/shard_map/slice | solution.py:118
  184.2 10.1 %multiply_subtract_fusion.2 = (f32[65536]{0:T(1024)}, f32[65536]{0:T(1024)}) fusion(f32[65536]{0:T(1024)S(1)} %bitcast.287, f32[]{:T(128)S(6)} %div.2722, f32[]{:T(128)S(6)} %div.2719, f32[]{:T(128)S(6)} %div.2716, f32[]{:T(128)S(6)} %div.2713, f32[]{:T(128)S(6)} %div.2710, f32[]{:T(128)S(6)} %div.2707, f32[]{:T(128)S(6)} %div.2704, f32[]{:T(128)S(6)} %div.2701, ...), kind=kLoop, calls=%fused_computation.16 | loop fusion | flops 4587520 | bytes 4456616 | tf_op jit(solution)/shard_map/sub | solution.py:24
  194.4 1.5 collective-permute-start
  195.9 1.8 fusion.40
  197.6 1.8 fusion.41
  199.4 1.8 fusion.42
  201.2 1.7 fusion.43
  202.9 1.8 fusion.44
  204.7 2.5 fusion.45
  207.2 1.7 stack.96
  208.9 1.7 constant_dynamic-update-slice_fusion.14
  210.6 1.7 stack.97
  212.3 1.7 stack.99
  214.0 1.7 stack.101
  215.7 1.7 stack.103
  217.3 1.7 stack.105
  219.1 1.7 constant_dynamic-update-slice_fusion.13
  220.7 1.7 constant_dynamic-update-slice_fusion.12
  222.4 1.7 constant_dynamic-update-slice_fusion.11
  224.1 0.7 constant_dynamic-update-slice_fusion.10
  224.8 1.7 constant_dynamic-update-slice_fusion.9
  226.5 6.2 %multiply_subtract_fusion.1 = f32[65536]{0:T(1024)} fusion(f32[65536]{0:T(1024)} %collective-permute-done, f32[65536]{0:T(1024)S(1)} %bitcast.289, f32[]{:T(128)} %bitcast.38, f32[]{:T(128)S(6)} %sub.3678, f32[65536]{0:T(1024)S(1)} %bitcast.271, f32[]{:T(128)S(6)} %sub.3676, f32[65536]{0:T(1024)S(1)} %bitcast.273, f32[]{:T(128)} %bitcast.33, f32[]{:T(128)} %bitcast.35, ...), kind=kLoop, calls=%fused_computation.15 | loop fusion | flops 1441792 | bytes 2621492 | tf_op jit(solution)/shard_map/sub | solution.py:118
  232.6 3.7 %all-to-all-start.2 = ((f32[1,16,4096]{2,0,1:T(1,128)}), f32[1,16,4096]{2,0,1:T(1,128)S(1)}, u32[]{:S(2)}, u32[]{:S(2)}) async-start(f32[1,16,4096]{2,0,1:T(1,128)} %bitcast.54), calls=%async_computation.2 | async-start | bytes 524288 | tf_op jit(solution)/shard_map/all_to_all | solution.py:122
  236.3 0.7 constant_dynamic-update-slice_fusion.8
  237.0 1.7 constant_dynamic-update-slice_fusion.7
  238.7 0.7 constant_dynamic-update-slice_fusion.6
  239.5 6.8 %all-to-all-done.2 = f32[1,16,4096]{2,0,1:T(1,128)S(1)} async-done(((f32[1,16,4096]{2,0,1:T(1,128)}), f32[1,16,4096]{2,0,1:T(1,128)S(1)}, u32[]{:S(2)}, u32[]{:S(2)}) %all-to-all-start.2) | async-done | bytes 262176 | tf_op jit(solution)/shard_map/all_to_all | solution.py:122
  246.3 9.5 %fusion.11 = (f32[1,4096]{1,0:T(1,128)S(1)}, f32[1,4096]{1,0:T(1,128)S(1)}, f32[1,4096]{1,0:T(1,128)S(1)}, f32[1,4096]{1,0:T(1,128)S(1)}, f32[1,4096]{1,0:T(1,12...) fusion(f32[1,16,4096]{2,0,1:T(1,128)S(1)} %all-to-all-done.2, ...), kind=kLoop, calls=%fused_computation.88 | loop fusion | flops 176128 | bytes 491636 | tf_op jit(solution)/shard_map/eval_jaxpr/div | solution.py:125
  255.7 0.9 multiply_subtract_fusion.16
  258.0 1.3 pad_maximum_fusion.1
  259.3 3.8 %all-to-all-start.3 = ((f32[2,16,4096]{2,0,1:T(2,128)}), f32[2,16,4096]{2,0,1:T(2,128)S(1)}, u32[]{:S(2)}, u32[]{:S(2)}) async-start(f32[2,16,4096]{2,0,1:T(2,128)} %pad_maximum_fusion.1), calls=%async_computation.3 | async-start | bytes 1048576 | tf_op jit(solution)/shard_map/all_to_all | solution.py:130
  263.1 0.7 constant_dynamic-update-slice_fusion.5
  263.9 0.7 constant_dynamic-update-slice_fusion.4
  264.7 0.7 constant_dynamic-update-slice_fusion.3
  265.4 0.7 constant_dynamic-update-slice_fusion.2
  266.1 0.7 constant_dynamic-update-slice_fusion.1
  266.8 0.7 constant_dynamic-update-slice_fusion
  267.6 9.5 %all-to-all-done.3 = f32[2,16,4096]{2,0,1:T(2,128)S(1)} async-done(((f32[2,16,4096]{2,0,1:T(2,128)}), f32[2,16,4096]{2,0,1:T(2,128)S(1)}, u32[]{:S(2)}, u32[]{:S(2)}) %all-to-all-start.3) | async-done | bytes 524320 | tf_op jit(solution)/shard_map/all_to_all | solution.py:130
  277.1 3.2 %fusion.4 = (f32[16,4096]{1,0:T(8,128)S(1)}, f32[16,4096]{1,0:T(8,128)S(1)}, f32[16,4096]{1,0:T(8,128)S(1)}) fusion(f32[2,16,4096]{2,0,1:T(2,128)S(1)} %all-to-all-done.3, f32[]{:T(128)} %bitcast.8, f32[]{:T(128)} %bitcast.35), kind=kLoop, calls=%fused_computation.12 | loop fusion | flops 131072 | bytes 1310728 | tf_op jit(solution)/shard_map/mul | solution.py:135
  280.5 3.2 %multiply_subtract_fusion = f32[15,128,512]{2,1,0:T(8,128)S(1)} fusion(f32[15,128,512]{2,1,0:T(8,128)} %constant_dynamic-update-slice_fusion, f32[15]{0:T(128)S(1)} %get-tuple-element.186, f32[128,512]{1,0:T(8,128)S(1)} %mul.4323, f32[15]{0:T(128)S(1)} %get-tuple-element.185, f32[128,512]{1,0:T(8,128)S(1)} %mul.4316), kind=kLoop, calls=%fused_computation.2 | loop fusion | flops 3932160 | bytes 8388728 | tf_op jit(solution)/shard_map/sub | solution.py:134
  283.7 2.7 pad_maximum_fusion
  (45 shorter events, 6.3 us)
Async XLA Ops:
  3.9 14.5 %all-to-all-start.1 = ((s32[32,1,8]{2,1,0:T(1,128)}), s32[32,1,8]{2,1,0:T(1,128)S(1)}, u32[]{:S(2)}, u32[]{:S(2)}) async-start(s32[32,1,8]{2,1,0:T(1,128)} %bitcast.4), calls=%async_computation.1 | async-start | bytes 32768 | tf_op jit(solution)/shard_map/all_to_all | solution.py:63
  12.1 12.2 %copy-start.5 = (f32[16]{0:T(128)S(1)}, f32[16]{0:T(128)}, u32[]{:S(2)}) copy-start(f32[16]{0:T(128)} %param.11) | copy-start | bytes 196
  12.1 40.5 %copy-start.3 = (f32[1,2]{0,1:T(2,128)S(1)}, f32[1,2]{0,1:T(2,128)}, u32[]{:S(2)}) copy-start(f32[1,2]{0,1:T(2,128)} %constant.203.clone.1) | copy-start | bytes 28
  16.9 44.4 %copy-start.4 = (f32[1,2]{0,1:T(2,128)S(1)}, f32[1,2]{0,1:T(2,128)}, u32[]{:S(2)}) copy-start(f32[1,2]{0,1:T(2,128)} %constant.201.clone.1) | copy-start | bytes 28
  18.4 130.7 %all-to-all-start = ((bf16[32,8,2048]{2,1,0:T(8,128)(2,1)}), bf16[32,8,2048]{2,1,0:T(8,128)(2,1)S(1)}, u32[]{:S(2)}, u32[]{:S(2)}) async-start(bf16[32,8,2048]{2,1,0:T(8,128)(2,1)} %fusion), calls=%async_computation | async-start | bytes 2097152 | tf_op jit(solution)/shard_map/all_to_all | solution.py:56
  65.7 13.4 %collective-permute-start.1 = (f32[2]{0:T(128)S(1)}, f32[2]{0:T(128)S(1)}, u32[]{:S(2)}, u32[]{:S(2)}) collective-permute-start(f32[2]{0:T(128)S(1)} %pad_maximum_fusion.2), channel_id=1, source_target_pairs={{2,0},{4,2},{6,4},{8,6},{10,8},{12,10},{14,12},{16,14},{18,16},{20... | collective-permute-start | bytes 32 | tf_op jit(solution)/shard_map/ppermute | solution.py:10
  68.7 7.3 %copy-start.6 = (u32[32]{0:T(128)S(1)}, u32[32]{0:T(128)}, u32[]{:S(2)}) copy-start(u32[32]{0:T(128)} %constant.208) | copy-start | bytes 388
  194.4 32.1 %collective-permute-start = (f32[65536]{0:T(1024)}, f32[65536]{0:T(1024)}, u32[]{:S(2)}, u32[]{:S(2)}) collective-permute-start(f32[65536]{0:T(1024)} %get-tuple-element.122), channel_id=1, source_target_pairs={{2,0},{4,2},{6,4},{8,6},{10,8},{12,10},{14,12},{16,14},{18,16},{20... | collective-permute-start | bytes 786440 | tf_op jit(solution)/shard_map/ppermute | solution.py:10
  232.6 30.5 %copy-start.1 = (f32[1,128,512]{2,1,0:T(8,128)S(1)}, f32[1,128,512]{2,1,0:T(8,128)}, u32[]{:S(2)}) copy-start(f32[1,128,512]{2,1,0:T(8,128)} %stack.105) | copy-start | bytes 786436
  232.6 13.6 %all-to-all-start.2 = ((f32[1,16,4096]{2,0,1:T(1,128)}), f32[1,16,4096]{2,0,1:T(1,128)S(1)}, u32[]{:S(2)}, u32[]{:S(2)}) async-start(f32[1,16,4096]{2,0,1:T(1,128)} %bitcast.54), calls=%async_computation.2 | async-start | bytes 524288 | tf_op jit(solution)/shard_map/all_to_all | solution.py:122
  236.3 27.6 %copy-start = (f32[65536]{0:T(1024)S(1)}, f32[65536]{0:T(1024)}, u32[]{:S(2)}) copy-start(f32[65536]{0:T(1024)} %get-tuple-element.52) | copy-start | bytes 786436
  237.0 26.9 %copy-start.2 = (f32[65536]{0:T(1024)S(1)}, f32[65536]{0:T(1024)}, u32[]{:S(2)}) copy-start(f32[65536]{0:T(1024)} %get-tuple-element.36) | copy-start | bytes 786436
  259.3 17.8 %all-to-all-start.3 = ((f32[2,16,4096]{2,0,1:T(2,128)}), f32[2,16,4096]{2,0,1:T(2,128)S(1)}, u32[]{:S(2)}, u32[]{:S(2)}) async-start(f32[2,16,4096]{2,0,1:T(2,128)} %pad_maximum_fusion.1), calls=%async_computation.3 | async-start | bytes 1048576 | tf_op jit(solution)/shard_map/all_to_all | solution.py:130
where the time goes:
time: 289 us; the launch traced here: 286 us
  other arithmetic  86 us (30%)
  between operations  65.1 us (23%)
  local copies, waits for them, and re-layouts  51.5 us (18%)
  blocking collectives  34.9 us (12%)
  starting transfers between devices  23.4 us (8%)
  waiting for transfers between devices  16.3 us (6%)
  matrix products  9.06 us (3%)
    sub x9, other arithmetic, thomas(): result.append(values[row_index] - ratios[row_index] * result[-1])  40.2 us
    unnamed x1, blocking collectives  34.9 us
    unnamed x33, local copies, waits for them, and re-layouts  24.1 us
    another operation x10, local copies, waits for them, and re-layouts, thomas(): return jnp.stack(result[::-1])  11.1 us
    all_to_all x1, waiting for transfers between devices, per_device(): lax.all_to_all(solved_pairs, 'gx', split_axis=1, concat_axis=2, tiled=True)  9.53 us
    div x1, other arithmetic, per_device(): lax.linalg.tridiagonal_solve(split_coef[:, 0], split_coef[:, 1], split_co...  9.47 us
    div x1, other arithmetic, thomas(): (right_side[row_index] - below_diag[row_index] * values[-1]) / pivot_value  8.72 us
    all_to_all x1, starting transfers between devices, per_device(): lax.all_to_all(out_slots.reshape(devices, capacity), ('gx', 'gy'), split_...  7.33 us
  transfers between devices with their start and end apart: 6, of which 2 were waited for; matrix products, arithmetic and copies ran while one was open for 24% of the time, Pallas kernels for 0%

commit v1 on v0

--- a/solution.py
+++ b/solution.py
@@ -1,7 +1,18 @@
+import functools
 import jax
 import jax.numpy as jnp
 from jax import lax
 from jax.sharding import PartitionSpec as P
+from jax.lax import all_to_all, axis_size
+
+
+def point_sizes(z, a_name):
+    return jnp.concatenate(
+        all_to_all(jnp.stack(jnp.split(z, axis_size(a_name), axis=1)), a_name, 0, 0), axis=0
+    )
+
+
+produce_stages_all = functools.partial(point_sizes, a_name="gx")
 
 
 def passed_along(x, axis, by):
@@ -119,9 +130,7 @@
     )
     coefficients = jnp.stack([lower_coef, center_coef, upper_coef])
     split_coef = lax.all_gather(coefficients, "gx", axis=0, tiled=True).reshape(-1, 3)
-    sides = lax.all_to_all(
-        reduced_side.reshape(1, grid_x, -1), "gx", split_axis=1, concat_axis=0, tiled=True
-    )[:, 0, :]
+    sides = produce_stages_all(reduced_side.reshape(1, grid_x, -1))[:, 0, :]
     separators = lax.linalg.tridiagonal_solve(
         split_coef[:, 0], split_coef[:, 1], split_coef[:, 2], sides
     )

time: 289 us -> 299 us (1.035)
  local copies, waits for them, and re-layouts: 51.5 us -> 62.2 us
    unnamed x33 -> x48, local copies, waits for them, and re-layouts: 24.1 us -> 33.3 us
  transfers between devices with their start and end apart: 6 -> 6, of which waited for: 2 -> 2; matrix products, arithmetic and copies ran while one was open for 24% -> 23% of each run, Pallas kernels for 0% -> 0%
where the time goes in v1:
time: 299 us; the launch traced here: 297 us
  other arithmetic  85.8 us (29%)
  between operations  65 us (22%)
  local copies, waits for them, and re-layouts  62.2 us (21%)
  blocking collectives  34.9 us (12%)
  starting transfers between devices  23.4 us (8%)
  waiting for transfers between devices  16.3 us (5%)
  matrix products  9.06 us (3%)
    sub x9, other arithmetic, thomas(): result.append(values[row_index] - ratios[row_index] * result[-1])  40 us
    unnamed x1, blocking collectives  34.9 us
    unnamed x48, local copies, waits for them, and re-layouts  33.3 us
    another operation x10, local copies, waits for them, and re-layouts, thomas(): return jnp.stack(result[::-1])  11.1 us
    div x1, other arithmetic, per_device(): lax.linalg.tridiagonal_solve(split_coef[:, 0], split_coef[:, 1], split_co...  9.58 us
    all_to_all x1, waiting for transfers between devices, per_device(): lax.all_to_all(solved_pairs, 'gx', split_axis=1, concat_axis=2, tiled=True)  9.53 us
    div x1, other arithmetic, thomas(): (right_side[row_index] - below_diag[row_index] * values[-1]) / pivot_value  8.61 us
    all_to_all x1, starting transfers between devices, per_device(): lax.all_to_all(out_slots.reshape(devices, capacity), ('gx', 'gy'), split_...  7.33 us
  transfers between devices with their start and end apart: 6, of which 2 were waited for; matrix products, arithmetic and copies ran while one was open for 23% of the time, Pallas kernels for 0%

profile of v1, /device:TPU:0, one launch (start us, length us, event | category | flops | bytes accessed | tf_op | source)
XLA Modules:
  0.0 296.8 jit_solution(10901846355051893225)
XLA Ops:
  0.0 0.7 fusion.7
  0.9 0.8 select_reduce_fusion.1
  2.4 0.8 convert_reduce_fusion
  3.9 7.3 %all-to-all-start.1 = ((s32[32,1,8]{2,1,0:T(1,128)}), s32[32,1,8]{2,1,0:T(1,128)S(1)}, u32[]{:S(2)}, u32[]{:S(2)}) async-start(s32[32,1,8]{2,1,0:T(1,128)} %bitcast.4), calls=%async_computation.1 | async-start | bytes 32768 | tf_op jit(solution)/shard_map/all_to_all | solution.py:74
  11.3 0.8 copy.18
  12.1 4.8 %fusion.70 = bf16[128,1,2048]{2,1,0:T(2,128)(2,1)S(1)} fusion(bf16[128,16,1]{1,2,0:T(2,128)(2,1)S(1)} %copy.18, bf16[128,16,2048]{2,1,0:T(8,128)(2,1)} %param.13), kind=kOutput, calls=%fused_computation.229 | convolution fusion | flops 8388608 | bytes 8916992 | tf_op jit(solution)/shard_map/bm,bmt->bt/dot_general | solution.py:45
  16.9 1.5 fusion
  18.4 5.8 %all-to-all-start = ((bf16[32,8,2048]{2,1,0:T(8,128)(2,1)}), bf16[32,8,2048]{2,1,0:T(8,128)(2,1)S(1)}, u32[]{:S(2)}, u32[]{:S(2)}) async-start(bf16[32,8,2048]{2,1,0:T(8,128)(2,1)} %fusion), calls=%async_computation | async-start | bytes 2097152 | tf_op jit(solution)/shard_map/all_to_all | solution.py:67
  24.3 0.7 fusion.69
  25.0 0.7 fusion.68
  52.3 8.6 %subtract_divide_fusion.29 = (f32[1,2]{0,1:T(2,128)S(1)}, f32[1,2]{0,1:T(2,128)S(1)}, f32[1,2]{0,1:T(2,128)S(1)}, f32[1,2]{0,1:T(2,128)S(1)}, f32[1,2]{0,1:T(2,1...) fusion(f32[]{:T(128)S(6)} %sub.3676, ...), kind=kLoop, calls=%fused_computation.192 | loop fusion | flops 80 | bytes 220 | tf_op jit(solution)/shard_map/div | solution.py:32
  60.9 1.2 multiply_subtract_fusion.31
  65.2 1.3 collective-permute-start.1
  68.2 6.6 %copy.20 = f32[2,8,128,512]{3,1,2,0:T(8,128)} copy(f32[2,8,128,512]{3,2,1,0:T(8,128)} %bitcast.329) | data formatting | bytes 8388608
  81.4 34.9 %all-reduce.1 = f32[48]{0:T(128)S(1)} all-reduce(f32[48]{0:T(128)S(1)} %maximum_dynamic-update-slice_fusion), channel_id=1, replica_groups=mesh['gx'=16,'gy'=2] {'gx'}, use_global_device_ids=true, to_apply=%add.1 | all-reduce | flops 48 | bytes 384
  117.1 0.7 fusion.63
  134.8 0.7 fusion.62
  148.0 0.7 reduce.66
  149.1 2.7 convolution_bitcast_fusion
  151.8 5.3 %copy.16 = f32[16,512,128]{2,1,0:T(8,128)} copy(f32[16,512,128]{1,2,0:T(8,128)} %convolution_bitcast_fusion) | data formatting | bytes 8388608 | tf_op jit(solution)/shard_map/pr,rxs->xps/transpose | solution.py:86
  157.2 6.0 %bitcast_add_fusion = f32[16,65536]{1,0:T(8,128)S(1)} fusion(f32[16,65536]{1,0:T(8,128)} %bitcast.327, f32[2,8,512,128]{3,2,1,0:T(8,128)} %bitcast.328), kind=kLoop, calls=%fused_computation | loop fusion | flops 1048576 | bytes 12582912 | tf_op jit(solution)/shard_map/add | solution.py:92
  163.1 17.5 %fusion.39 = (f32[65536]{0:T(1024)}, f32[1,65536]{1,0:T(1,128)S(1)}, f32[1,65536]{1,0:T(1,128)S(1)}, f32[1,65536]{1,0:T(1,128)S(1)}, f32[1,65536]{1,0:T(1,128)S(...) fusion(f32[]{:T(128)S(6)} %div.2722, ...), kind=kLoop, calls=%fused_computation.213 | loop fusion | flops 2949120 | bytes 8126584 | tf_op jit(solution)/shard_map/sub | solution.py:35
  180.6 3.3 %fusion.61 = (f32[1,65536]{1,0:T(1,128)S(1)}, f32[1,65536]{1,0:T(1,128)S(1)}, f32[1,65536]{1,0:T(1,128)S(1)}, f32[1,65536]{1,0:T(1,128)S(1)}, f32[1,65536]{1,0:T...) fusion(f32[16,65536]{1,0:T(8,128)S(1)} %bitcast_add_fusion), kind=kLoop, calls=%fused_computation.220 | loop fusion | bytes 7864320 | tf_op jit(solution)/shard_map/slice | solution.py:129
  183.9 10.0 %multiply_subtract_fusion.2 = (f32[65536]{0:T(1024)}, f32[65536]{0:T(1024)}) fusion(f32[65536]{0:T(1024)S(1)} %bitcast.349, f32[]{:T(128)S(6)} %div.2722, f32[]{:T(128)S(6)} %div.2719, f32[]{:T(128)S(6)} %div.2716, f32[]{:T(128)S(6)} %div.2713, f32[]{:T(128)S(6)} %div.2710, f32[]{:T(128)S(6)} %div.2707, f32[]{:T(128)S(6)} %div.2704, f32[]{:T(128)S(6)} %div.2701, ...), kind=kLoop, calls=%fused_computation.16 | loop fusion | flops 4587520 | bytes 4456616 | tf_op jit(solution)/shard_map/sub | solution.py:35
  193.8 1.5 collective-permute-start
  195.3 1.8 fusion.40
  197.1 1.8 fusion.41
  198.9 1.8 fusion.42
  200.6 1.7 fusion.43
  202.4 1.8 fusion.44
  204.1 2.5 fusion.45
  206.7 1.7 stack.147
  208.3 1.7 constant_dynamic-update-slice_fusion.14
  210.0 1.7 stack.148
  211.7 1.7 stack.150
  213.4 1.7 stack.152
  215.1 1.7 stack.154
  216.8 1.7 stack.156
  218.5 1.7 constant_dynamic-update-slice_fusion.13
  220.2 1.7 constant_dynamic-update-slice_fusion.12
  221.8 1.7 constant_dynamic-update-slice_fusion.11
  223.5 0.7 constant_dynamic-update-slice_fusion.10
  224.2 1.7 constant_dynamic-update-slice_fusion.9
  225.9 6.2 %multiply_subtract_fusion.1 = f32[65536]{0:T(1024)} fusion(f32[65536]{0:T(1024)} %collective-permute-done, f32[65536]{0:T(1024)S(1)} %bitcast.351, f32[]{:T(128)} %bitcast.38, f32[]{:T(128)S(6)} %sub.3678, f32[65536]{0:T(1024)S(1)} %bitcast.333, f32[]{:T(128)S(6)} %sub.3676, f32[65536]{0:T(1024)S(1)} %bitcast.335, f32[]{:T(128)} %bitcast.33, f32[]{:T(128)} %bitcast.35, ...), kind=kLoop, calls=%fused_computation.15 | loop fusion | flops 1441792 | bytes 2621492 | tf_op jit(solution)/shard_map/sub | solution.py:129
  232.1 1.0 reshape.1836
  242.9 3.7 %all-to-all-start.2 = ((f32[16,1,1,4096]{3,2,1,0:T(1,128)}), f32[16,1,1,4096]{3,2,1,0:T(1,128)S(1)}, u32[]{:S(2)}, u32[]{:S(2)}) async-start(f32[16,1,1,4096]{3,2,1,0:T(1,128)} %constant_dynamic-update-slice_fusion.15), calls=%async_computation.2 | async-start | bytes 524288 | tf_op jit(solution)/shard_map/all_to_all | solution.py:11
  246.6 0.7 constant_dynamic-update-slice_fusion.8
  247.3 1.7 constant_dynamic-update-slice_fusion.7
  249.0 0.7 constant_dynamic-update-slice_fusion.6
  249.7 6.8 %all-to-all-done.2 = f32[16,1,1,4096]{3,2,1,0:T(1,128)S(1)} async-done(((f32[16,1,1,4096]{3,2,1,0:T(1,128)}), f32[16,1,1,4096]{3,2,1,0:T(1,128)S(1)}, u32[]{:S(2)}, u32[]{:S(2)}) %all-to-all-start.2) | async-done | bytes 262176 | tf_op jit(solution)/shard_map/all_to_all | solution.py:11
  256.5 9.6 %fusion.11 = (f32[1,4096]{1,0:T(1,128)S(1)}, f32[1,4096]{1,0:T(1,128)S(1)}, f32[1,4096]{1,0:T(1,128)S(1)}, f32[1,4096]{1,0:T(1,128)S(1)}, f32[1,4096]{1,0:T(1,12...) fusion(f32[16,1,1,4096]{3,2,1,0:T(1,128)S(1)} %all-to-all-done., ...), kind=kLoop, calls=%fused_computation.104 | loop fusion | flops 176128 | bytes 491636 | tf_op jit(solution)/shard_map/eval_jaxpr/div | solution.py:134
  266.1 0.9 multiply_subtract_fusion.16
  268.4 1.3 pad_maximum_fusion.1
  269.6 3.8 %all-to-all-start.3 = ((f32[2,16,4096]{2,0,1:T(2,128)}), f32[2,16,4096]{2,0,1:T(2,128)S(1)}, u32[]{:S(2)}, u32[]{:S(2)}) async-start(f32[2,16,4096]{2,0,1:T(2,128)} %pad_maximum_fusion.1), calls=%async_computation.3 | async-start | bytes 1048576 | tf_op jit(solution)/shard_map/all_to_all | solution.py:139
  273.5 0.7 constant_dynamic-update-slice_fusion.5
  274.3 0.7 constant_dynamic-update-slice_fusion.4
  275.1 0.7 constant_dynamic-update-slice_fusion.3
  275.8 0.7 constant_dynamic-update-slice_fusion.2
  276.5 0.7 constant_dynamic-update-slice_fusion.1
  277.2 0.7 constant_dynamic-update-slice_fusion
  277.9 9.5 %all-to-all-done.3 = f32[2,16,4096]{2,0,1:T(2,128)S(1)} async-done(((f32[2,16,4096]{2,0,1:T(2,128)}), f32[2,16,4096]{2,0,1:T(2,128)S(1)}, u32[]{:S(2)}, u32[]{:S(2)}) %all-to-all-start.3) | async-done | bytes 524320 | tf_op jit(solution)/shard_map/all_to_all | solution.py:139
  287.5 3.2 %fusion.4 = (f32[16,4096]{1,0:T(8,128)S(1)}, f32[16,4096]{1,0:T(8,128)S(1)}, f32[16,4096]{1,0:T(8,128)S(1)}) fusion(f32[2,16,4096]{2,0,1:T(2,128)S(1)} %all-to-all-done.3, f32[]{:T(128)} %bitcast.8, f32[]{:T(128)} %bitcast.35), kind=kLoop, calls=%fused_computation.12 | loop fusion | flops 131072 | bytes 1310728 | tf_op jit(solution)/shard_map/mul | solution.py:144
  290.9 3.2 %multiply_subtract_fusion = f32[15,128,512]{2,1,0:T(8,128)S(1)} fusion(f32[15,128,512]{2,1,0:T(8,128)} %constant_dynamic-update-slice_fusion, f32[15]{0:T(128)S(1)} %get-tuple-element.186, f32[128,512]{1,0:T(8,128)S(1)} %mul.4323, f32[15]{0:T(128)S(1)} %get-tuple-element.185, f32[128,512]{1,0:T(8,128)S(1)} %mul.4316), kind=kLoop, calls=%fused_computation.2 | loop fusion | flops 3932160 | bytes 8388728 | tf_op jit(solution)/shard_map/sub | solution.py:143
  294.0 2.7 pad_maximum_fusion
  (62 shorter events, 16.8 us)
Async XLA Ops:
  3.9 14.5 %all-to-all-start.1 = ((s32[32,1,8]{2,1,0:T(1,128)}), s32[32,1,8]{2,1,0:T(1,128)S(1)}, u32[]{:S(2)}, u32[]{:S(2)}) async-start(s32[32,1,8]{2,1,0:T(1,128)} %bitcast.4), calls=%async_computation.1 | async-start | bytes 32768 | tf_op jit(solution)/shard_map/all_to_all | solution.py:74
  12.1 12.2 %copy-start.5 = (f32[16]{0:T(128)S(1)}, f32[16]{0:T(128)}, u32[]{:S(2)}) copy-start(f32[16]{0:T(128)} %param.11) | copy-start | bytes 196
  12.1 40.2 %copy-start.3 = (f32[1,2]{0,1:T(2,128)S(1)}, f32[1,2]{0,1:T(2,128)}, u32[]{:S(2)}) copy-start(f32[1,2]{0,1:T(2,128)} %constant.203.clone.1) | copy-start | bytes 28
  16.9 44.0 %copy-start.4 = (f32[1,2]{0,1:T(2,128)S(1)}, f32[1,2]{0,1:T(2,128)}, u32[]{:S(2)}) copy-start(f32[1,2]{0,1:T(2,128)} %constant.201.clone.1) | copy-start | bytes 28
  18.4 130.4 %all-to-all-start = ((bf16[32,8,2048]{2,1,0:T(8,128)(2,1)}), bf16[32,8,2048]{2,1,0:T(8,128)(2,1)S(1)}, u32[]{:S(2)}, u32[]{:S(2)}) async-start(bf16[32,8,2048]{2,1,0:T(8,128)(2,1)} %fusion), calls=%async_computation | async-start | bytes 2097152 | tf_op jit(solution)/shard_map/all_to_all | solution.py:67
  65.2 13.7 %collective-permute-start.1 = (f32[2]{0:T(128)S(1)}, f32[2]{0:T(128)S(1)}, u32[]{:S(2)}, u32[]{:S(2)}) collective-permute-start(f32[2]{0:T(128)S(1)} %pad_maximum_fusion.2), channel_id=1, source_target_pairs={{2,0},{4,2},{6,4},{8,6},{10,8},{12,10},{14,12},{16,14},{18,16},{20... | collective-permute-start | bytes 32 | tf_op jit(solution)/shard_map/ppermute | solution.py:21
  68.2 7.3 %copy-start.6 = (u32[32]{0:T(128)S(1)}, u32[32]{0:T(128)}, u32[]{:S(2)}) copy-start(u32[32]{0:T(128)} %constant.208) | copy-start | bytes 388
  193.8 32.1 %collective-permute-start = (f32[65536]{0:T(1024)}, f32[65536]{0:T(1024)}, u32[]{:S(2)}, u32[]{:S(2)}) collective-permute-start(f32[65536]{0:T(1024)} %get-tuple-element.122), channel_id=1, source_target_pairs={{2,0},{4,2},{6,4},{8,6},{10,8},{12,10},{14,12},{16,14},{18,16},{20... | collective-permute-start | bytes 786440 | tf_op jit(solution)/shard_map/ppermute | solution.py:21
  242.9 30.6 %copy-start.1 = (f32[1,128,512]{2,1,0:T(8,128)S(1)}, f32[1,128,512]{2,1,0:T(8,128)}, u32[]{:S(2)}) copy-start(f32[1,128,512]{2,1,0:T(8,128)} %stack.156) | copy-start | bytes 786436
  242.9 13.6 %all-to-all-start.2 = ((f32[16,1,1,4096]{3,2,1,0:T(1,128)}), f32[16,1,1,4096]{3,2,1,0:T(1,128)S(1)}, u32[]{:S(2)}, u32[]{:S(2)}) async-start(f32[16,1,1,4096]{3,2,1,0:T(1,128)} %constant_dynamic-update-slice_fusion.15), calls=%async_computation.2 | async-start | bytes 524288 | tf_op jit(solution)/shard_map/all_to_all | solution.py:11
  246.6 27.7 %copy-start = (f32[65536]{0:T(1024)S(1)}, f32[65536]{0:T(1024)}, u32[]{:S(2)}) copy-start(f32[65536]{0:T(1024)} %get-tuple-element.52) | copy-start | bytes 786436
  247.3 27.0 %copy-start.2 = (f32[65536]{0:T(1024)S(1)}, f32[65536]{0:T(1024)}, u32[]{:S(2)}) copy-start(f32[65536]{0:T(1024)} %get-tuple-element.36) | copy-start | bytes 786436
  269.6 17.8 %all-to-all-start.3 = ((f32[2,16,4096]{2,0,1:T(2,128)}), f32[2,16,4096]{2,0,1:T(2,128)S(1)}, u32[]{:S(2)}, u32[]{:S(2)}) async-start(f32[2,16,4096]{2,0,1:T(2,128)} %pad_maximum_fusion.1), calls=%async_computation.3 | async-start | bytes 1048576 | tf_op jit(solution)/shard_map/all_to_all | solution.py:139
